TPU v7x, 32 devices: a whole 2x2x4 slice. The times are simulated.
32 devices in a mesh: dp: 4 (over x, core), half: 2 (over y), own: 4 (over z).
Axes of the slice: x: 2, y: 2, z: 4, core: 2. Of those that a mesh axis runs over, the one named last changes fastest.
Arguments:
- grad_parts: bfloat16 [4, 6, 1024, 1024], P('dp', None, ('half', 'own')), may hold values from -6 to 6
- owner_table: int32 [6, 1], replicated, may hold values from 0 to 3; in each aligned block of 6 rows (0 to 5, 6 to 11, ...) at most 2 rows name the same one
- left_basis: bfloat16 [8, 1024, 1024], P(('half', 'own')), may hold values from -0.1875 to 0.1875
- right_basis: bfloat16 [8, 1024, 1024], P(('half', 'own')), may hold values from -0.1875 to 0.1875
- first_moment: bfloat16 [8, 1024, 1024], P(('half', 'own'), 'dp'), may hold values from -6 to 6
- second_moment: bfloat16 [8, 1024, 1024], P(('half', 'own'), 'dp'), may hold values from 0.5 to 8
Outputs:
- update: bfloat16 [6, 1024, 1024], P(None, ('half', 'own'), 'dp')
Inputs may be any that keep to these rules, and one draw needn't show every extreme that they name: `owner_table`: every owner index is named by at least one block and by at most 2 blocks; some owner is named by exactly 2 blocks.
All inputs are finite; a program needn't handle non-finite values.
Results may differ from a plain program's by a relative error of at most 0.013.
Values may be sent and summed in bfloat16 or wider, within the bound.
A program may use at most 128 MiB of HBM per device.

v0:
```python
import jax
import jax.numpy as jnp
from jax import lax
from jax.sharding import PartitionSpec as P

beta_first = 0.9
beta_second = 0.95
bias_first = 1.0 - 0.9**10
bias_second = 1.0 - 0.95**10
epsilon = 1e-08


def slot_select(owner_table, owner_count, slot_count):
    owner_ids = owner_table[:, 0]
    positions = jnp.arange(owner_ids.shape[0], dtype=jnp.int32)
    shared = (owner_ids[:, None] == owner_ids[None, :]) & (positions[None, :] < positions[:, None])
    ranking = jnp.sum(shared.astype(jnp.int32), axis=1)
    slot_ids = ranking * owner_count + owner_ids
    slot_range = jnp.arange(slot_count, dtype=jnp.int32)
    return (slot_range[:, None] == slot_ids[None, :]).astype(jnp.bfloat16)


def local(grad_parts, owner_table, left_basis, right_basis, first_moment, second_moment):
    halves = lax.axis_size("half")
    owners = lax.axis_size("own")
    replicas = lax.axis_size("dp")
    block_count = grad_parts.shape[1]
    piece_rows = grad_parts.shape[2]
    block_width = grad_parts.shape[3]
    quarter = block_width // replicas
    offset = lax.axis_index("dp") * quarter
    summed = lax.psum_scatter(
        grad_parts[0].astype(jnp.float32).astype(jnp.bfloat16),
        "dp",
        scatter_dimension=2,
        tiled=True,
    )
    selector = slot_select(owner_table, owners, halves * owners)
    flat_grad = summed.reshape(block_count, piece_rows * quarter)
    packed = jnp.dot(selector, flat_grad, preferred_element_type=jnp.float32).astype(jnp.bfloat16)
    packed = packed.reshape(halves, owners, piece_rows, quarter)
    arrived = lax.all_to_all(
        lax.all_to_all(packed, "half", split_axis=0, concat_axis=0, tiled=True),
        "own",
        split_axis=1,
        concat_axis=1,
        tiled=True,
    )
    grad_block = arrived.reshape(block_width, quarter)
    left_matrix = left_basis[0]
    right_matrix = right_basis[0]
    right_rows = lax.dynamic_slice_in_dim(right_matrix, offset, quarter, 0)
    left_slice = lax.dynamic_slice_in_dim(left_matrix, offset, quarter, 1)
    projected = lax.dot_general(
        left_slice,
        lax.all_gather(grad_block, "dp", axis=1, tiled=True),
        (((0,), (0,)), ((), ())),
        preferred_element_type=jnp.float32,
    )
    rotated = jnp.dot(
        projected.astype(jnp.bfloat16), right_matrix, preferred_element_type=jnp.float32
    )
    first_new = beta_first * first_moment[0].astype(jnp.float32) + (1.0 - beta_first) * rotated
    second_new = (
        beta_second * second_moment[0].astype(jnp.float32) + (1.0 - beta_second) * rotated * rotated
    )
    direction = (first_new / bias_first / (jnp.sqrt(second_new / bias_second) + epsilon)).astype(
        jnp.bfloat16
    )
    partial_cols = lax.dot_general(
        lax.all_gather(direction, "dp", axis=0, tiled=True),
        right_rows,
        (((1,), (1,)), ((), ())),
        preferred_element_type=jnp.float32,
    )
    update_block = jnp.dot(
        left_matrix, partial_cols.astype(jnp.bfloat16), preferred_element_type=jnp.float32
    )
    outgoing = update_block.astype(jnp.bfloat16).reshape(halves, owners, piece_rows, quarter)
    returned = lax.all_to_all(
        lax.all_to_all(outgoing, "half", split_axis=0, concat_axis=0, tiled=True),
        "own",
        split_axis=1,
        concat_axis=1,
        tiled=True,
    )
    flat_back = returned.reshape(halves * owners, piece_rows * quarter)
    placed = lax.dot_general(
        selector, flat_back, (((0,), (0,)), ((), ())), preferred_element_type=jnp.float32
    )
    return placed.astype(jnp.bfloat16).reshape(block_count, piece_rows, quarter)


def solution(mesh):
    return jax.shard_map(
        local,
        mesh=mesh,
        in_specs=(
            P("dp", None, ("half", "own"), None),
            P(),
            P(("half", "own"), None, None),
            P(("half", "own"), None, None),
            P(("half", "own"), "dp", None),
            P(("half", "own"), "dp", None),
        ),
        out_specs=P(None, ("half", "own"), "dp"),
        check_vma=False,
    )
```

profile of v0, /device:TPU:0, one launch (start us, length us, event | category | flops | bytes accessed | tf_op | source)
XLA Modules:
  0.0 161.1 jit_solution(16821739264425904918)
XLA Ops:
  6.5 0.0 copy-start
  6.5 0.0 reduce-scatter.2.cloned.1.call-start
  6.5 0.7 reduce-scatter.2.cloned.1.call-update
  7.3 0.0 all-gather.3.cloned.1.call-start
  7.3 0.9 convert_reduce_fusion
  8.2 0.7 multiply_add_fusion
  8.9 31.8 %reduce-scatter.2.cloned.1.call-done = bf16[6,128,256]{2,1,0:T(8,128)(2,1)} async-done(((bf16[6,128,1024]{2,1,0:T(8,128)(2,1)}), bf16[6,128,256]{2,1,0:T(8,128)(2,1)}) %reduce-scatter.2.cloned.1.call-update) | async-done | bytes 393232 | tf_op jit(solution)/shard_map/reduce_scatter | solution.py:32
  40.7 1.2 copy.26
  41.9 0.3 convolution_convert_fusion.1
  42.2 0.1 copy.27
  42.3 10.5 %all_to_all.20 = bf16[2,4,128,256]{3,2,1,0:T(8,128)(2,1)S(1)} all-to-all(bf16[2,4,128,256]{3,2,1,0:T(8,128)(2,1)S(1)} %bitcast.60), channel_id=1, replica_groups=mesh['dp'=4,'half'=2,'own'=4] {'half'}, dimensions={0} | all-to-all | bytes 1048576 | tf_op jit(solution)/shard_map/all_to_all | solution.py:43
  52.8 0.0 copy-start.1
  52.8 0.0 copy-start.2
  52.8 17.9 %all_to_all.21 = bf16[2,4,128,256]{3,2,0,1:T(8,128)(2,1)S(1)} all-to-all(bf16[2,4,128,256]{3,2,0,1:T(8,128)(2,1)S(1)} %copy.20), channel_id=1, replica_groups=mesh['dp'=4,'half'=2,'own'=4] {'own'}, dimensions={1} | all-to-all | bytes 1048576 | tf_op jit(solution)/shard_map/all_to_all | solution.py:42
  70.7 0.8 copy.21
  71.6 0.0 all-gather.3.cloned.1.call-update
  71.6 0.0 all-gather.5.cloned.1.call-start
  71.6 20.2 %all-gather.3.cloned.1.call-done = bf16[1024,1024]{1,0:T(8,128)(2,1)} async-done(((bf16[1024,256]{1,0:T(8,128)(2,1)}), bf16[1024,1024]{1,0:T(8,128)(2,1)}) %all-gather.3.cloned.1.call-update) | async-done | bytes 2097168 | tf_op jit(solution)/shard_map/all_gather | solution.py:56
  91.8 0.0 copy-done
  91.8 0.0 copy-done.1
  91.8 0.0 copy-done.2
  91.8 5.0 %fusion.16 = bf16[256,1024]{1,0:T(8,128)(2,1)} fusion(bf16[1,256,1024]{2,1,0:T(8,128)(2,1)S(1)} %copy-done.1, bf16[1,256,1024]{2,1,0:T(8,128)(2,1)S(1)} %copy-done.2, bf16[1,1024,1024]{2,1,0:T(8,128)(2,1)} %param.9, bf16[1024,1024]{1,0:T(8,128)(2,1)} %all-gather.3.cloned.1.call-done, bf16[1,1024,1024]{2,1,0:T(8,128)(2,1)S(1)} %copy-done, s32[]{:T(128)S(6)} %select_n.4), kind=kOutput, calls=%fused_computation.18 | convolution fusion | flops 1077673984 | bytes 6291460 | tf_op jit(solution)/shard_map/dot_general | solution.py:60
  96.8 0.0 all-gather.5.cloned.1.call-update
  96.8 22.7 %all-gather.5.cloned.1.call-done = bf16[1024,1024]{1,0:T(8,128)(2,1)} async-done(((bf16[256,1024]{1,0:T(8,128)(2,1)}), bf16[1024,1024]{1,0:T(8,128)(2,1)}) %all-gather.5.cloned.1.call-update) | async-done | bytes 2097168 | tf_op jit(solution)/shard_map/all_gather | solution.py:71
  119.5 4.0 %fusion.7 = bf16[1024,256]{0,1:T(8,128)(2,1)S(1)} fusion(bf16[1,1024,1024]{2,1,0:T(8,128)(2,1)S(1)} %copy-done, bf16[1024,1024]{1,0:T(8,128)(2,1)} %all-gather.5.cloned.1.call-done, bf16[1,1024,1024]{2,1,0:T(8,128)(2,1)} %param.9, s32[]{:T(128)S(6)} %select_n.4), kind=kOutput, calls=%fused_computation.10 | convolution fusion | flops 1074266112 | bytes 5242884 | tf_op jit(solution)/shard_map/dot_general | solution.py:76
  123.5 0.2 copy.25
  123.7 11.1 %all_to_all.22 = bf16[2,4,128,256]{3,2,1,0:T(8,128)(2,1)S(1)} all-to-all(bf16[2,4,128,256]{3,2,1,0:T(8,128)(2,1)S(1)} %bitcast.61), channel_id=1, replica_groups=mesh['dp'=4,'half'=2,'own'=4] {'half'}, dimensions={0} | all-to-all | bytes 1048576 | tf_op jit(solution)/shard_map/all_to_all | solution.py:81
  134.8 18.3 %all_to_all.23 = bf16[2,4,128,256]{3,2,0,1:T(8,128)(2,1)S(1)} all-to-all(bf16[2,4,128,256]{3,2,0,1:T(8,128)(2,1)S(1)} %copy.23), channel_id=1, replica_groups=mesh['dp'=4,'half'=2,'own'=4] {'own'}, dimensions={1} | all-to-all | bytes 1048576 | tf_op jit(solution)/shard_map/all_to_all | solution.py:80
  153.1 0.3 copy.28
  153.4 0.4 convolution_convert_fusion
  153.8 0.8 copy.31
  (3 shorter events, 0.1 us)
Async XLA Ops:
  6.5 85.3 %copy-start = (bf16[1,1024,1024]{2,1,0:T(8,128)(2,1)S(1)}, bf16[1,1024,1024]{2,1,0:T(8,128)(2,1)}, u32[]{:S(2)}) copy-start(bf16[1,1024,1024]{2,1,0:T(8,128)(2,1)} %param.8) | copy-start | bytes 6291460
  6.5 34.1 %reduce-scatter.2.cloned.1.call-start = ((), (), s32[]{:S(2)}) async-start(), calls=%async_computation.5 | async-start | bytes 1966080 | tf_op jit(solution)/shard_map/reduce_scatter | solution.py:32
  7.3 84.6 %all-gather.3.cloned.1.call-start = ((), (), s32[]{:S(2)}) async-start(), calls=%async_computation.6 | async-start | bytes 2621440 | tf_op jit(solution)/shard_map/all_gather | solution.py:56
  52.8 39.0 %copy-start.1 = (bf16[1,256,1024]{2,1,0:T(8,128)(2,1)S(1)}, bf16[1,256,1024]{2,1,0:T(8,128)(2,1)}, u32[]{:S(2)}) copy-start(bf16[1,256,1024]{2,1,0:T(8,128)(2,1)} %param.11) | copy-start | bytes 1572868
  52.8 39.0 %copy-start.2 = (bf16[1,256,1024]{2,1,0:T(8,128)(2,1)S(1)}, bf16[1,256,1024]{2,1,0:T(8,128)(2,1)}, u32[]{:S(2)}) copy-start(bf16[1,256,1024]{2,1,0:T(8,128)(2,1)} %param.10) | copy-start | bytes 1572868
  71.6 47.9 %all-gather.5.cloned.1.call-start = ((), (), s32[]{:S(2)}) async-start(), calls=%async_computation.7 | async-start | bytes 2621440 | tf_op jit(solution)/shard_map/all_gather | solution.py:71
Sparse Core Ops, SparseCore 0:
  9.9 30.7 reduce-scatter.1
  71.7 20.0 all-gather.2
  96.9 22.5 all-gather.4
where the time goes:
time: 162 us; the launch traced here: 161 us
  waiting for transfers between devices  75.4 us (47%)
  blocking collectives  57.7 us (36%)
  between operations  13.2 us (8%)
  matrix products  9.55 us (6%)
  local copies, waits for them, and re-layouts  3.59 us (2%)
    reduce_scatter x1, waiting for transfers between devices, local(): lax.psum_scatter(grad_parts[0].astype(jnp.float32).astype(jnp.bfloat16),...  31.8 us
    all_gather x1, waiting for transfers between devices, local(): lax.all_gather(direction, 'dp', axis=0, tiled=True)  22.7 us
    all_gather x1, waiting for transfers between devices, local(): lax.all_gather(grad_block, 'dp', axis=1, tiled=True)  20.2 us
    all_to_all x1, blocking collectives, local(): lax.all_to_all(lax.all_to_all(outgoing, 'half', split_axis=0, concat_axis...  18.3 us
    all_to_all x1, blocking collectives, local(): lax.all_to_all(lax.all_to_all(packed, 'half', split_axis=0, concat_axis=0...  17.9 us
    all_to_all x1, blocking collectives, local(): lax.all_to_all(outgoing, 'half', split_axis=0, concat_axis=0, tiled=True)  11.1 us
    all_to_all x1, blocking collectives, local(): lax.all_to_all(packed, 'half', split_axis=0, concat_axis=0, tiled=True)  10.5 us
    dot_general x1, matrix products, local(): jnp.dot(projected.astype(jnp.bfloat16), right_matrix, preferred_element_t...  4.95 us
  transfers between devices with their start and end apart: 3, of which 3 were waited for; matrix products, arithmetic and copies ran while one was open for 1% of the time, Pallas kernels for 0%

commit v1 on v0

--- a/solution.py
+++ b/solution.py
@@ -8,6 +8,30 @@
 bias_first = 1.0 - 0.9**10
 bias_second = 1.0 - 0.95**10
 epsilon = 1e-08
+
+
+def enter_edges(sample, row_axis):
+    next_value, frame_out, view_out = (
+        lax.axis_size(row_axis),
+        lax.axis_index(row_axis),
+        sample.shape[0],
+    )
+    met_up, everything = (sample, 1)
+    while everything < next_value:
+        met_up = jnp.concatenate(
+            [
+                met_up,
+                lax.ppermute(
+                    met_up,
+                    axis_name=row_axis,
+                    perm=tuple(((d, (d - everything) % next_value) for d in range(next_value))),
+                ),
+            ],
+            axis=0,
+        )
+        everything = 2 * everything
+    latest = jnp.roll(met_up, frame_out * view_out, axis=0)
+    return latest
 
 
 def slot_select(owner_table, owner_count, slot_count):
@@ -68,7 +92,7 @@
         jnp.bfloat16
     )
     partial_cols = lax.dot_general(
-        lax.all_gather(direction, "dp", axis=0, tiled=True),
+        enter_edges(direction, "dp"),
         right_rows,
         (((1,), (1,)), ((), ())),
         preferred_element_type=jnp.float32,

time: 162 us -> 180 us (1.11)
  local copies, waits for them, and re-layouts: 3.59 us -> 10.6 us
  waiting for transfers between devices: 75.4 us -> 82.3 us
  starting transfers between devices: 0.08 us -> 1.93 us
    ppermute x0 -> x2, waiting for transfers between devices: none -> 29.5 us  [enter_edges(): lax.ppermute(met_up, axis_name=row_axis, perm=tuple(((d, (d - everything)...]
    all_gather x1 -> x0, waiting for transfers between devices: 22.7 us -> none  [local(): lax.all_gather(direction, 'dp', axis=0, tiled=True)]
    unnamed x10 -> x12, local copies, waits for them, and re-layouts: 2.45 us -> 7.24 us
    concatenate x0 -> x1, local copies, waits for them, and re-layouts: none -> 2.27 us  [enter_edges(): latest = jnp.roll(met_up, frame_out * view_out, axis=0)]
    ppermute x0 -> x2, starting transfers between devices: none -> 1.89 us  [enter_edges(): lax.ppermute(met_up, axis_name=row_axis, perm=tuple(((d, (d - everything)...]
  transfers between devices with their start and end apart: 3 -> 4, of which waited for: 3 -> 4; matrix products, arithmetic and copies ran while one was open for 1% -> 1% of each run, Pallas kernels for 0% -> 0%
where the time goes in v1:
time: 180 us; the launch traced here: 179 us
  waiting for transfers between devices  82.3 us (46%)
  blocking collectives  58.9 us (33%)
  between operations  13.5 us (8%)
  local copies, waits for them, and re-layouts  10.6 us (6%)
  matrix products  9.61 us (5%)
  other arithmetic  2.65 us (1%)
  starting transfers between devices  1.93 us (1%)
    reduce_scatter x1, waiting for transfers between devices, local(): lax.psum_scatter(grad_parts[0].astype(jnp.float32).astype(jnp.bfloat16),...  31.8 us
    ppermute x2, waiting for transfers between devices, enter_edges(): lax.ppermute(met_up, axis_name=row_axis, perm=tuple(((d, (d - everything)...  29.5 us
    all_gather x1, waiting for transfers between devices, local(): lax.all_gather(grad_block, 'dp', axis=1, tiled=True)  20.2 us
    all_to_all x1, blocking collectives, local(): lax.all_to_all(lax.all_to_all(outgoing, 'half', split_axis=0, concat_axis...  18.8 us
    all_to_all x1, blocking collectives, local(): lax.all_to_all(lax.all_to_all(packed, 'half', split_axis=0, concat_axis=0...  17.9 us
    all_to_all x1, blocking collectives, local(): lax.all_to_all(outgoing, 'half', split_axis=0, concat_axis=0, tiled=True)  11.7 us
    all_to_all x1, blocking collectives, local(): lax.all_to_all(packed, 'half', split_axis=0, concat_axis=0, tiled=True)  10.5 us
    unnamed x12, local copies, waits for them, and re-layouts  7.24 us
  transfers between devices with their start and end apart: 4, of which 4 were waited for; matrix products, arithmetic and copies ran while one was open for 1% of the time, Pallas kernels for 0%

profile of v1, /device:TPU:0, one launch (start us, length us, event | category | flops | bytes accessed | tf_op | source)
XLA Modules:
  0.0 179.5 jit_solution(849044435299132783)
XLA Ops:
  6.5 0.0 copy-start
  6.5 0.0 reduce-scatter.2.cloned.1.call-start
  6.5 0.7 reduce-scatter.2.cloned.1.call-update
  7.3 0.0 all-gather.2.cloned.1.call-start
  7.3 0.9 convert_reduce_fusion
  8.2 0.7 multiply_add_fusion
  8.9 31.8 %reduce-scatter.2.cloned.1.call-done = bf16[6,128,256]{2,1,0:T(8,128)(2,1)} async-done(((bf16[6,128,1024]{2,1,0:T(8,128)(2,1)}), bf16[6,128,256]{2,1,0:T(8,128)(2,1)}) %reduce-scatter.2.cloned.1.call-update) | async-done | bytes 393232 | tf_op jit(solution)/shard_map/reduce_scatter | solution.py:56
  40.7 1.2 copy.26
  41.9 0.3 convolution_convert_fusion.1
  42.2 0.1 copy.27
  42.3 10.5 %all_to_all.20 = bf16[2,4,128,256]{3,2,1,0:T(8,128)(2,1)S(1)} all-to-all(bf16[2,4,128,256]{3,2,1,0:T(8,128)(2,1)S(1)} %bitcast.63), channel_id=1, replica_groups=mesh['dp'=4,'half'=2,'own'=4] {'half'}, dimensions={0} | all-to-all | bytes 1048576 | tf_op jit(solution)/shard_map/all_to_all | solution.py:67
  52.8 0.0 copy-start.1
  52.8 17.9 %all_to_all.21 = bf16[2,4,128,256]{3,2,0,1:T(8,128)(2,1)S(1)} all-to-all(bf16[2,4,128,256]{3,2,0,1:T(8,128)(2,1)S(1)} %copy.20), channel_id=1, replica_groups=mesh['dp'=4,'half'=2,'own'=4] {'own'}, dimensions={1} | all-to-all | bytes 1048576 | tf_op jit(solution)/shard_map/all_to_all | solution.py:66
  70.7 0.8 copy.21
  71.5 0.0 all-gather.2.cloned.1.call-update
  71.6 20.2 %all-gather.2.cloned.1.call-done = bf16[1024,1024]{1,0:T(8,128)(2,1)} async-done(((bf16[1024,256]{1,0:T(8,128)(2,1)}), bf16[1024,1024]{1,0:T(8,128)(2,1)}) %all-gather.2.cloned.1.call-update) | async-done | bytes 2097168 | tf_op jit(solution)/shard_map/all_gather | solution.py:80
  91.8 0.0 copy-done
  91.8 0.0 copy-done.1
  91.8 5.0 %constant_dynamic-update-slice_fusion.5 = (bf16[2048,1024]{1,0:T(8,128)(2,1)}, bf16[256,1024]{1,0:T(8,128)(2,1)S(1)}) fusion(bf16[1,256,1024]{2,1,0:T(8,128)(2,1)S(1)} %copy-done.1, bf16[1,1024,1024]{2,1,0:T(8,128)(2,1)} %param.9, bf16[1024,1024]{1,0:T(8,128)(2,1)} %all-gather.2.cloned.1.call-done, bf16[1,1024,1024]{2,1,0:T(8,128)(2,1)S(1)} %copy-done, ...), kind=kOutput, calls=%fused_computation.32 | convolution fusion | flops 1077673984 | bytes 6815748 | tf_op jit(solution)/shard_map/dot_general | solution.py:84
  96.8 0.2 collective-permute-start
  97.0 6.7 %collective-permute-done = bf16[256,1024]{1,0:T(8,128)(2,1)S(1)} collective-permute-done((bf16[256,1024]{1,0:T(8,128)(2,1)S(1)}, bf16[256,1024]{1,0:T(8,128)(2,1)S(1)}, u32[]{:S(2)}, u32[]{:S(2)}) %collective-permute-start) | collective-permute-done | bytes 524320 | tf_op jit(solution)/shard_map/ppermute | solution.py:24
  103.7 1.1 pad_maximum_fusion
  104.8 1.7 collective-permute-start.1
  106.5 0.8 constant_dynamic-update-slice_fusion.4
  107.3 22.8 %collective-permute-done.1 = bf16[512,1024]{1,0:T(8,128)(2,1)} collective-permute-done((bf16[512,1024]{1,0:T(8,128)(2,1)}, bf16[512,1024]{1,0:T(8,128)(2,1)}, u32[]{:S(2)}, u32[]{:S(2)}) %collective-permute-start.1) | collective-permute-done | bytes 1048608 | tf_op jit(solution)/shard_map/ppermute | solution.py:24
  130.1 2.3 %constant_dynamic-update-slice_fusion.3 = bf16[2048,1024]{1,0:T(8,128)(2,1)} fusion(bf16[2048,1024]{1,0:T(8,128)(2,1)} %constant_dynamic-update-slice_fusion.4, bf16[512,1024]{1,0:T(8,128)(2,1)} %collective-permute-done.1), kind=kLoop, calls=%fused_computation.30 | loop fusion | bytes 2097152
  132.5 0.8 constant_dynamic-update-slice_fusion.2
  133.3 0.8 constant_dynamic-update-slice_fusion.1
  134.1 2.3 %constant_dynamic-update-slice_fusion = bf16[2048,1024]{1,0:T(8,128)(2,1)} fusion(bf16[2048,1024]{1,0:T(8,128)(2,1)} %constant_dynamic-update-slice_fusion.1, bf16[512,1024]{1,0:T(8,128)(2,1)} %collective-permute-done.1), kind=kLoop, calls=%fused_computation.27 | loop fusion | bytes 2097152 | tf_op jit(solution)/shard_map/jit(_roll_dynamic)/concatenate | solution.py:33
  136.4 4.0 %fusion.12 = bf16[1024,256]{0,1:T(8,128)(2,1)S(1)} fusion(bf16[1,1024,1024]{2,1,0:T(8,128)(2,1)S(1)} %copy-done, bf16[2048,1024]{1,0:T(8,128)(2,1)} %constant_dynamic-update-slice_fusion, s32[]{:T(128)S(6)} %select_n.19, bf16[1,1024,1024]{2,1,0:T(8,128)(2,1)} %param.9, s32[]{:T(128)S(6)} %select_n.17), kind=kOutput, calls=%fused_computation.12 | convolution fusion | flops 1074266112 | bytes 5242888 | tf_op jit(solution)/shard_map/dot_general | solution.py:100
  140.4 0.2 copy.25
  140.6 11.7 %all_to_all.22 = bf16[2,4,128,256]{3,2,1,0:T(8,128)(2,1)S(1)} all-to-all(bf16[2,4,128,256]{3,2,1,0:T(8,128)(2,1)S(1)} %bitcast.64), channel_id=1, replica_groups=mesh['dp'=4,'half'=2,'own'=4] {'half'}, dimensions={0} | all-to-all | bytes 1048576 | tf_op jit(solution)/shard_map/all_to_all | solution.py:105
  152.3 18.8 %all_to_all.23 = bf16[2,4,128,256]{3,2,0,1:T(8,128)(2,1)S(1)} all-to-all(bf16[2,4,128,256]{3,2,0,1:T(8,128)(2,1)S(1)} %copy.23), channel_id=1, replica_groups=mesh['dp'=4,'half'=2,'own'=4] {'own'}, dimensions={1} | all-to-all | bytes 1048576 | tf_op jit(solution)/shard_map/all_to_all | solution.py:104
  171.2 0.3 copy.28
  171.5 0.4 convolution_convert_fusion
  171.8 0.8 copy.31
  (3 shorter events, 0.1 us)
Async XLA Ops:
  6.5 85.3 %copy-start = (bf16[1,1024,1024]{2,1,0:T(8,128)(2,1)S(1)}, bf16[1,1024,1024]{2,1,0:T(8,128)(2,1)}, u32[]{:S(2)}) copy-start(bf16[1,1024,1024]{2,1,0:T(8,128)(2,1)} %param.8) | copy-start | bytes 6291460
  6.5 34.1 %reduce-scatter.2.cloned.1.call-start = ((), (), s32[]{:S(2)}) async-start(), calls=%async_computation.5 | async-start | bytes 1966080 | tf_op jit(solution)/shard_map/reduce_scatter | solution.py:56
  7.3 84.5 %all-gather.2.cloned.1.call-start = ((), (), s32[]{:S(2)}) async-start(), calls=%async_computation.6 | async-start | bytes 2621440 | tf_op jit(solution)/shard_map/all_gather | solution.py:80
  52.8 39.0 %copy-start.1 = (bf16[1,256,1024]{2,1,0:T(8,128)(2,1)S(1)}, bf16[1,256,1024]{2,1,0:T(8,128)(2,1)}, u32[]{:S(2)}) copy-start(bf16[1,256,1024]{2,1,0:T(8,128)(2,1)} %param.11) | copy-start | bytes 1572868
  96.8 6.9 %collective-permute-start = (bf16[256,1024]{1,0:T(8,128)(2,1)S(1)}, bf16[256,1024]{1,0:T(8,128)(2,1)S(1)}, u32[]{:S(2)}, u32[]{:S(2)}) collective-permute-start(bf16[256,1024]{1,0:T(8,128)(2,1)S(1)} %get-tuple-element.6), channel_id=1, source_target_pairs={{0,24},{8,0},{16,8},{24,16},{1,25},{9,1},{17,9},{25,17},{2,26},{10... | collective-permute-start | bytes 1572872 | tf_op jit(solution)/shard_map/ppermute | solution.py:24
  104.8 25.4 %collective-permute-start.1 = (bf16[512,1024]{1,0:T(8,128)(2,1)}, bf16[512,1024]{1,0:T(8,128)(2,1)}, u32[]{:S(2)}, u32[]{:S(2)}) collective-permute-start(bf16[512,1024]{1,0:T(8,128)(2,1)} %pad_maximum_fusion), channel_id=1, source_target_pairs={{0,16},{8,24},{16,0},{24,8},{1,17},{9,25},{17,1},{25,9},{2,18},{10... | collective-permute-start | bytes 3145736 | tf_op jit(solution)/shard_map/ppermute | solution.py:24
Sparse Core Ops, SparseCore 0:
  9.9 30.7 reduce-scatter.1
  71.7 20.0 all-gather.1
